TPU v7x, 32 devices: a whole 2x2x4 slice. The times are simulated.
32 devices in a mesh: blk: 16 (over z, y, core), uly: 2 (over x).
Axes of the slice: x: 2, y: 2, z: 4, core: 2. Of those that a mesh axis runs over, the one named last changes fastest.
Arguments:
- footage_probes: bfloat16 [1024, 32, 64], P(('blk', 'uly')), may hold values from -6 to 6
- footage_lookup_keys: bfloat16 [1024, 32, 64], P(('blk', 'uly')), may hold values from -6 to 6
- footage_payload: bfloat16 [1024, 32, 64], P(('blk', 'uly')), may hold values from -6 to 6
- caption_probes: bfloat16 [256, 32, 64], replicated, may hold values from -6 to 6
- caption_lookup_keys: bfloat16 [256, 32, 64], replicated, may hold values from -6 to 6
- caption_payload: bfloat16 [256, 32, 64], replicated, may hold values from -6 to 6
- footage_probes_amplitude: float32 [64], replicated, may hold values from 0.25 to 1.75
- footage_keys_amplitude: float32 [64], replicated, may hold values from 0.25 to 1.75
- caption_probes_amplitude: float32 [64], replicated, may hold values from 0.25 to 1.75
- caption_keys_amplitude: float32 [64], replicated, may hold values from 0.25 to 1.75
- focus_sharpness: float32 [32], replicated, may hold values from 1.5 to 4
- caption_validity: int32 [256], replicated, may hold values 0 or 1
Outputs:
- vid_out: bfloat16 [1024, 32, 64], P(('blk', 'uly'))
- txt_out: bfloat16 [256, 32, 64], P('uly', 'blk')
Inputs may be any that keep to these rules, and one draw needn't show every extreme that they name: caption_validity holds only 0 and 1.
All inputs are finite; a program needn't handle non-finite values.
Results may differ from a plain program's by a relative error of at most 0.0035.
Values may be sent and summed in bfloat16 or wider, within the bound.
A program may use at most 64 MiB of HBM per device.

v0:
```python
import math
import jax
import jax.numpy as jnp
from jax import lax
from jax.sharding import PartitionSpec as P

EPSILON = 1e-06
NEGATIVE = -1e30


def normed(tensor, gain_vector, rescale_factor):
    widened = tensor.astype(jnp.float32)
    inverse = lax.rsqrt(jnp.mean(widened * widened, axis=-1, keepdims=True) + EPSILON)
    return (widened * inverse * gain_vector * rescale_factor).astype(jnp.bfloat16)


def fragment_contributions(queries, key_rows, value_rows, valid):
    scores = jnp.einsum("qhd,khd->hqk", queries, key_rows, preferred_element_type=jnp.float32)
    if valid is not None:
        scores = jnp.where(valid[None, None, :], scores, NEGATIVE)
    maxima = jnp.max(scores, axis=-1)
    weights = jnp.exp(scores - maxima[..., None])
    if valid is not None:
        weights = jnp.where(valid[None, None, :], weights, 0.0)
    totals = jnp.sum(weights, axis=-1)
    accum = jnp.einsum(
        "hqk,khd->hqd", weights, value_rows.astype(jnp.float32), precision=lax.Precision.HIGHEST
    )
    return (maxima, totals, accum)


def combine(earlier, later):
    max_one, total_one, accum_one = earlier
    max_two, total_two, accum_two = later
    merged_max = jnp.maximum(max_one, max_two)
    factor_one = jnp.exp(max_one - merged_max)
    factor_two = jnp.exp(max_two - merged_max)
    merged_total = total_one * factor_one + total_two * factor_two
    merged_accum = accum_one * factor_one[..., None] + accum_two * factor_two[..., None]
    return (merged_max, merged_total, merged_accum)


def on_device(
    footage_probes,
    footage_lookup_keys,
    footage_payload,
    caption_probes,
    caption_lookup_keys,
    caption_payload,
    footage_probes_amplitude,
    footage_keys_amplitude,
    caption_probes_amplitude,
    caption_keys_amplitude,
    focus_sharpness,
    caption_validity,
):
    channel_width = footage_probes.shape[2]
    rescale_factor = focus_sharpness[None, :, None] / math.sqrt(channel_width)
    q_norm = normed(footage_probes, footage_probes_amplitude, rescale_factor)
    k_norm = normed(footage_lookup_keys, footage_keys_amplitude, 1.0)
    q_local = lax.all_to_all(q_norm, "blk", split_axis=1, concat_axis=0, tiled=True)
    k_local = lax.all_to_all(k_norm, "blk", split_axis=1, concat_axis=0, tiled=True)
    v_local = lax.all_to_all(footage_payload, "blk", split_axis=1, concat_axis=0, tiled=True)
    local_heads = q_local.shape[1]
    head_start = lax.axis_index("blk") * local_heads
    local_scale = lax.dynamic_slice_in_dim(rescale_factor, head_start, local_heads, 1)
    text_q = normed(
        lax.dynamic_slice_in_dim(caption_probes, head_start, local_heads, 1),
        caption_probes_amplitude,
        local_scale,
    )
    text_k = normed(
        lax.dynamic_slice_in_dim(caption_lookup_keys, head_start, local_heads, 1),
        caption_keys_amplitude,
        1.0,
    )
    text_v = lax.dynamic_slice_in_dim(caption_payload, head_start, local_heads, 1)
    text_valid = caption_validity == 1
    text_share = caption_probes.shape[0] // lax.axis_size("uly")
    row_start = lax.axis_index("uly") * text_share
    video_rows = q_local.shape[0]
    queries = jnp.concatenate(
        [q_local, lax.dynamic_slice_in_dim(text_q, row_start, text_share, 0)], 0
    )

    def fold_inward(running, gathered):
        key_block, value_block = gathered
        row_count = key_block.shape[0]
        block_rows = math.gcd(row_count, 512)

        def absorb_block(block_index, running_state):
            key_part = lax.dynamic_slice_in_dim(key_block, block_index * block_rows, block_rows, 0)
            value_part = lax.dynamic_slice_in_dim(
                value_block, block_index * block_rows, block_rows, 0
            )
            return combine(
                running_state, fragment_contributions(queries, key_part, value_part, None)
            )

        return lax.fori_loop(0, row_count // block_rows, absorb_block, running)

    first_state = fragment_contributions(queries, text_k, text_v, text_valid)
    maxima, totals, accum = fold_inward(
        first_state,
        (
            lax.all_gather(k_local, "uly", axis=0, tiled=True),
            lax.all_gather(v_local, "uly", axis=0, tiled=True),
        ),
    )
    attended = jnp.transpose(accum / totals[..., None], (1, 0, 2)).astype(jnp.bfloat16)
    vid_out = lax.all_to_all(attended[:video_rows], "blk", split_axis=0, concat_axis=1, tiled=True)
    txt_out = attended[video_rows:]
    return (vid_out, txt_out)


def solution(mesh):
    return jax.shard_map(
        on_device,
        mesh=mesh,
        in_specs=(
            P(("blk", "uly"), None, None),
            P(("blk", "uly"), None, None),
            P(("blk", "uly"), None, None),
            P(),
            P(),
            P(),
            P(),
            P(),
            P(),
            P(),
            P(),
            P(),
        ),
        out_specs=(P(("blk", "uly"), None, None), P("uly", "blk", None)),
        check_vma=False,
    )
```

profile of v0, /device:TPU:0, one launch (start us, length us, event | category | flops | bytes accessed | tf_op | source)
XLA Modules:
  0.0 76.9 jit_solution(12764766947317799488)
XLA Ops:
  0.6 0.0 copy-start
  0.6 0.0 copy-start.1
  0.7 0.0 copy-start.3
  0.7 0.8 broadcast_multiply_fusion
  1.4 1.2 %fusion.21 = f32[32,32]{0,1:T(8,128)S(1)} fusion(bf16[32,32,64]{2,1,0:T(8,128)(2,1)} %param.14), kind=kLoop, calls=%fused_computation.27 | loop fusion | flops 195584 | bytes 135168 | tf_op jit(solution)/shard_map/reduce_sum | solution.py:13
  2.6 1.2 %fusion.44 = bf16[32,32,64]{2,1,0:T(8,128)(2,1)S(1)} fusion(f32[32]{0:T(128)S(1)} %broadcast_multiply_fusion, f32[64]{0:T(128)} %param.20, f32[32,32]{0,1:T(8,128)S(1)} %add_rsqrt_fusion.1, bf16[32,32,64]{2,1,0:T(8,128)(2,1)} %param.14), kind=kLoop, calls=%fused_computation.64 | loop fusion | flops 327680 | bytes 266624
  3.8 0.0 copy-start.2
  3.8 0.9 %reshape.50 = bf16[16,2,2048]{2,1,0:T(2,128)(2,1)} reshape(bf16[32,32,64]{2,1,0:T(8,128)(2,1)S(1)} %fusion.44) | data formatting | bytes 262144
  4.7 7.4 %all-to-all-start = ((bf16[16,2,2048]{2,1,0:T(2,128)(2,1)}), bf16[16,2,2048]{2,1,0:T(2,128)(2,1)S(1)}, u32[]{:S(2)}, u32[]{:S(2)}) async-start(bf16[16,2,2048]{2,1,0:T(2,128)(2,1)} %reshape.50), calls=%async_computation | async-start | bytes 262144 | tf_op jit(solution)/shard_map/all_to_all | solution.py:61
  12.2 0.9 %fusion.28 = (f32[256,2]{0,1:T(2,128)S(1)}, f32[256,2]{0,1:T(2,128)S(1)}) fusion(bf16[256,32,64]{0,2,1:T(8,128)(2,1)} %param.18, s32[]{:T(128)S(6)} %select_n.24, bf16[256,32,64]{0,2,1:T(8,128)(2,1)} %param.17), kind=kLoop, calls=%fused_computation.38 | loop fusion | flops 195584 | bytes 135172 | tf_op jit(solution)/shard_map/reduce_sum | solution.py:13
  13.1 0.0 copy-done.1
  13.1 0.0 copy-start.4
  13.1 0.2 fusion.25
  13.4 0.0 copy-done.3
  13.4 0.0 copy-start.6
  13.4 0.2 fusion.43
  13.6 0.9 %dynamic-slice_convert_fusion = f32[256,2,64]{0,2,1:T(8,128)S(1)} fusion(bf16[256,32,64]{0,2,1:T(8,128)(2,1)} %param.17, s32[]{:T(128)S(6)} %select_n.24), kind=kLoop, calls=%fused_computation.49 | loop fusion | flops 32768 | bytes 196612 | tf_op jit(solution)/shard_map/convert_element_type | solution.py:12
  14.5 0.9 %reshape.52 = bf16[16,2,2048]{2,1,0:T(2,128)(2,1)} reshape(bf16[32,32,64]{2,1,0:T(8,128)(2,1)S(1)} %fusion.43) | data formatting | bytes 262144
  15.3 4.7 %all-to-all-done = bf16[16,2,2048]{2,1,0:T(2,128)(2,1)S(1)} async-done(((bf16[16,2,2048]{2,1,0:T(2,128)(2,1)}), bf16[16,2,2048]{2,1,0:T(2,128)(2,1)S(1)}, u32[]{:S(2)}, u32[]{:S(2)}) %all-to-all-start) | async-done | bytes 131104 | tf_op jit(solution)/shard_map/all_to_all | solution.py:61
  20.1 3.5 %all-to-all-start.1 = ((bf16[16,2,2048]{2,1,0:T(2,128)(2,1)}), bf16[16,2,2048]{2,1,0:T(2,128)(2,1)S(1)}, u32[]{:S(2)}, u32[]{:S(2)}) async-start(bf16[16,2,2048]{2,1,0:T(2,128)(2,1)} %reshape.52), calls=%async_computation.1 | async-start | bytes 262144 | tf_op jit(solution)/shard_map/all_to_all | solution.py:62
  23.6 0.1 dynamic_slice.30
  23.7 0.0 copy-done.2
  23.7 0.1 copy.72
  23.8 0.9 %reshape.54 = bf16[16,2,2048]{2,1,0:T(2,128)(2,1)} reshape(bf16[32,32,64]{2,1,0:T(8,128)(2,1)S(1)} %bitcast.58) | data formatting | bytes 262144
  24.7 0.0 copy-done.4
  24.7 0.1 fusion.34
  24.8 6.7 %all-to-all-done.1 = bf16[16,2,2048]{2,1,0:T(2,128)(2,1)S(1)} async-done(((bf16[16,2,2048]{2,1,0:T(2,128)(2,1)}), bf16[16,2,2048]{2,1,0:T(2,128)(2,1)S(1)}, u32[]{:S(2)}, u32[]{:S(2)}) %all-to-all-start.1) | async-done | bytes 131104 | tf_op jit(solution)/shard_map/all_to_all | solution.py:62
  31.4 3.5 %all-to-all-start.2 = ((bf16[16,2,2048]{2,1,0:T(2,128)(2,1)}), bf16[16,2,2048]{2,1,0:T(2,128)(2,1)S(1)}, u32[]{:S(2)}, u32[]{:S(2)}) async-start(bf16[16,2,2048]{2,1,0:T(2,128)(2,1)} %reshape.54), calls=%async_computation.2 | async-start | bytes 262144 | tf_op jit(solution)/shard_map/all_to_all | solution.py:63
  35.0 0.0 copy-done.6
  35.0 0.2 reshape.51
  35.2 0.1 copy.45
  35.4 0.2 reshape.53
  35.6 9.2 %all_gather.6 = bf16[1024,2,64]{2,0,1:T(8,128)(2,1)S(1)} all-gather(bf16[512,2,64]{2,0,1:T(8,128)(2,1)S(1)} %bitcast.50), channel_id=1, replica_groups=mesh['blk'=16,'uly'=2] {'uly'}, dimensions={0}, use_global_device_ids=true | all-gather | bytes 393216 | tf_op jit(solution)/shard_map/all_gather | solution.py:106
  44.8 0.2 copy.51
  45.0 0.0 all-to-all-done.2
  45.0 0.2 reshape.55
  45.2 0.0 copy-start.5
  45.2 8.3 %all_gather.7 = bf16[1024,2,64]{2,0,1:T(8,128)(2,1)S(1)} all-gather(bf16[512,2,64]{2,0,1:T(8,128)(2,1)S(1)} %bitcast.51), channel_id=1, replica_groups=mesh['blk'=16,'uly'=2] {'uly'}, dimensions={0}, use_global_device_ids=true | all-gather | bytes 393216 | tf_op jit(solution)/shard_map/all_gather | solution.py:107
  53.5 0.2 copy.52
  53.8 0.0 copy-done.5
  53.8 1.3 %fusion.42 = (f32[2,640]{1,0:T(2,128)S(1)}, f32[2,640,256]{1,2,0:T(8,128)S(1)}) fusion(f32[64]{0:T(128)S(1)} %copy-done.5, f32[256,2]{0,1:T(2,128)S(1)} %add_rsqrt_fusion.2, bf16[256,32,64]{0,2,1:T(8,128)(2,1)} %param.18, s32[]{:T(128)S(6)} %select_n.24, bf16[128,2,64]{0,2,1:T(8,128)(2,1)S(1)} %fusion.34, bf16[512,2,64]{0,2,1:T(8,128)(2,1)S(1)} %copy.45, ...), kind=kOutput, calls=%fused_computation.61 | convolution fusion | flops 43055872 | bytes 1547780 | tf_op jit(solution)/shard_map/qhd,khd->hqk/dot_general | solution.py:18
  55.1 0.3 fusion.17
  55.3 0.0 copy-done
  55.4 0.8 %fusion.16 = f32[2,640,64]{1,2,0:T(8,128)S(1)} fusion(f32[2,640,256]{1,2,0:T(8,128)S(1)} %get-tuple-element.177, f32[2,640]{1,0:T(2,128)S(1)} %get-tuple-element.236, pred[256]{0:T(512)(128)(4,1)S(1)} %broadcast_compare_fusion, bf16[256,32,64]{0,2,1:T(8,128)(2,1)S(1)} %copy-done, s32[]{:T(128)S(6)} %select_n.24), kind=kOutput, calls=%fused_computation.18 | convolution fusion | flops 252313600 | bytes 1709572 | tf_op jit(solution)/shard_map/hqk,khd->hqd/dot_general | solution.py:26
  56.2 4.7 %while.17 = (s32[]{:T(128)}, f32[2,640]{1,0:T(2,128)S(1)}, f32[2,640]{1,0:T(2,128)S(1)}, f32[2,640,64]{1,2,0:T(8,128)S(1)}, bf16[1024,2,64]{0,2,1:T(8,128)(2,1)S...) while((s32[]{:T(128)}, f32[2,640]{1,0:T(2,128)S(1)}, ...), condition=%wide.region_9.10_spmd, body=%wide.region_6.9_spmd.sunk | while | flops 590074880 | bytes 9017507 | solution.py:100
  56.2 0.6 bitcast_reduce_fusion.2
  56.8 0.4 fusion.54
  57.2 1.4 %fusion.55 = f32[2,640,64]{1,2,0:T(8,128)S(1)} fusion(f32[2,512,640]{2,1,0:T(8,128)S(1)} %get-tuple-element.229, f32[2,640]{1,0:T(2,128)S(1)} %get-tuple-element.230, f32[2,640,64]{1,2,0:T(8,128)S(1)} %get-tuple-element.249, f32[2,640]{1,0:T(2,128)S(1)} %get-tuple-element.233, f32[2,640]{1,0:T(2,128)S(1)} %get-tuple-element.234, ...), kind=kOutput, calls=%fused_computation.7.clone.1 | convolution fusion | flops 504217600 | bytes 3423236 | tf_op jit(solution)/shard_map/while/body/eval_jaxpr/hqk,khd->hqd/dot_general | solution.py:26
  58.5 0.6 bitcast_reduce_fusion.2
  59.1 0.4 fusion.54
  59.5 1.3 %fusion.55 = f32[2,640,64]{1,2,0:T(8,128)S(1)} fusion(f32[2,512,640]{2,1,0:T(8,128)S(1)} %get-tuple-element.229, f32[2,640]{1,0:T(2,128)S(1)} %get-tuple-element.230, f32[2,640,64]{1,2,0:T(8,128)S(1)} %get-tuple-element.249, f32[2,640]{1,0:T(2,128)S(1)} %get-tuple-element.233, f32[2,640]{1,0:T(2,128)S(1)} %get-tuple-element.234, ...), kind=kOutput, calls=%fused_computation.7.clone.1 | convolution fusion | flops 504217600 | bytes 3423236 | tf_op jit(solution)/shard_map/while/body/eval_jaxpr/hqk,khd->hqd/dot_general | solution.py:26
  60.9 0.2 copy.55
  61.1 0.2 slice.8
  61.3 0.9 %reshape.56 = bf16[16,2,2048]{2,1,0:T(2,128)(2,1)} reshape(bf16[512,2,64]{2,1,0:T(2,128)(2,1)S(1)} %slice.8) | data formatting | bytes 262144
  62.2 5.6 %all-to-all-start.3 = ((bf16[16,2,2048]{2,1,0:T(2,128)(2,1)}), bf16[16,2,2048]{2,1,0:T(2,128)(2,1)S(1)}, u32[]{:S(2)}, u32[]{:S(2)}) async-start(bf16[16,2,2048]{2,1,0:T(2,128)(2,1)} %reshape.56), calls=%async_computation.3 | async-start | bytes 262144 | tf_op jit(solution)/shard_map/all_to_all | solution.py:111
  67.9 0.7 copy.59
  68.6 7.1 %all-to-all-done.3 = bf16[16,2,2048]{2,1,0:T(2,128)(2,1)S(1)} async-done(((bf16[16,2,2048]{2,1,0:T(2,128)(2,1)}), bf16[16,2,2048]{2,1,0:T(2,128)(2,1)S(1)}, u32[]{:S(2)}, u32[]{:S(2)}) %all-to-all-start.3) | async-done | bytes 131104 | tf_op jit(solution)/shard_map/all_to_all | solution.py:111
  75.8 0.2 reshape.57
  76.1 0.8 %copy.58 = bf16[32,32,64]{2,1,0:T(8,128)(2,1)} copy(bf16[32,32,64]{2,0,1:T(8,128)(2,1)S(1)} %bitcast.57) | data formatting | bytes 262144
  (16 shorter events, 0.3 us)
Async XLA Ops:
  0.6 54.7 %copy-start = (bf16[256,32,64]{0,2,1:T(8,128)(2,1)S(1)}, bf16[256,32,64]{0,2,1:T(8,128)(2,1)}, u32[]{:S(2)}) copy-start(bf16[256,32,64]{0,2,1:T(8,128)(2,1)} %param.19) | copy-start | bytes 3145732
  0.6 12.4 %copy-start.1 = (bf16[32,32,64]{2,1,0:T(8,128)(2,1)S(1)}, bf16[32,32,64]{2,1,0:T(8,128)(2,1)}, u32[]{:S(2)}) copy-start(bf16[32,32,64]{2,1,0:T(8,128)(2,1)} %param.15) | copy-start | bytes 393220
  0.7 12.7 %copy-start.3 = (f32[64]{0:T(128)S(1)}, f32[64]{0:T(128)}, u32[]{:S(2)}) copy-start(f32[64]{0:T(128)} %param.21) | copy-start | bytes 772
  3.8 19.9 %copy-start.2 = (bf16[32,32,64]{2,1,0:T(8,128)(2,1)S(1)}, bf16[32,32,64]{2,1,0:T(8,128)(2,1)}, u32[]{:S(2)}) copy-start(bf16[32,32,64]{2,1,0:T(8,128)(2,1)} %param.16) | copy-start | bytes 393220
  4.7 15.3 %all-to-all-start = ((bf16[16,2,2048]{2,1,0:T(2,128)(2,1)}), bf16[16,2,2048]{2,1,0:T(2,128)(2,1)S(1)}, u32[]{:S(2)}, u32[]{:S(2)}) async-start(bf16[16,2,2048]{2,1,0:T(2,128)(2,1)} %reshape.50), calls=%async_computation | async-start | bytes 262144 | tf_op jit(solution)/shard_map/all_to_all | solution.py:61
  13.1 11.6 %copy-start.4 = (f32[64]{0:T(128)S(1)}, f32[64]{0:T(128)}, u32[]{:S(2)}) copy-start(f32[64]{0:T(128)} %param.22) | copy-start | bytes 772
  13.4 21.6 %copy-start.6 = (s32[256]{0:T(256)S(1)}, s32[256]{0:T(256)}, u32[]{:S(2)}) copy-start(s32[256]{0:T(256)} %param.25) | copy-start | bytes 3076
  20.1 11.4 %all-to-all-start.1 = ((bf16[16,2,2048]{2,1,0:T(2,128)(2,1)}), bf16[16,2,2048]{2,1,0:T(2,128)(2,1)S(1)}, u32[]{:S(2)}, u32[]{:S(2)}) async-start(bf16[16,2,2048]{2,1,0:T(2,128)(2,1)} %reshape.52), calls=%async_computation.1 | async-start | bytes 262144 | tf_op jit(solution)/shard_map/all_to_all | solution.py:62
  31.4 13.5 %all-to-all-start.2 = ((bf16[16,2,2048]{2,1,0:T(2,128)(2,1)}), bf16[16,2,2048]{2,1,0:T(2,128)(2,1)S(1)}, u32[]{:S(2)}, u32[]{:S(2)}) async-start(bf16[16,2,2048]{2,1,0:T(2,128)(2,1)} %reshape.54), calls=%async_computation.2 | async-start | bytes 262144 | tf_op jit(solution)/shard_map/all_to_all | solution.py:63
  45.2 8.6 %copy-start.5 = (f32[64]{0:T(128)S(1)}, f32[64]{0:T(128)}, u32[]{:S(2)}) copy-start(f32[64]{0:T(128)} %param.23) | copy-start | bytes 772
  62.2 13.6 %all-to-all-start.3 = ((bf16[16,2,2048]{2,1,0:T(2,128)(2,1)}), bf16[16,2,2048]{2,1,0:T(2,128)(2,1)S(1)}, u32[]{:S(2)}, u32[]{:S(2)}) async-start(bf16[16,2,2048]{2,1,0:T(2,128)(2,1)} %reshape.56), calls=%async_computation.3 | async-start | bytes 262144 | tf_op jit(solution)/shard_map/all_to_all | solution.py:111
where the time goes:
time: 77.5 us; the launch traced here: 76.9 us
  starting transfers between devices  20.1 us (26%)
  waiting for transfers between devices  18.5 us (24%)
  blocking collectives  17.5 us (23%)
  local copies, waits for them, and re-layouts  7.24 us (9%)
  other arithmetic  6.54 us (8%)
  matrix products  5.96 us (8%)
  between operations  1 us (1%)
    all_gather x1, blocking collectives, on_device(): lax.all_gather(k_local, 'uly', axis=0, tiled=True)  9.16 us
    all_gather x1, blocking collectives, on_device(): lax.all_gather(v_local, 'uly', axis=0, tiled=True)  8.3 us
    all_to_all x1, starting transfers between devices, on_device(): lax.all_to_all(q_norm, 'blk', split_axis=1, concat_axis=0, tiled=True)  7.41 us
    all_to_all x1, waiting for transfers between devices, on_device(): lax.all_to_all(attended[:video_rows], 'blk', split_axis=0, concat_axis=1,...  7.13 us
    all_to_all x1, waiting for transfers between devices, on_device(): lax.all_to_all(k_norm, 'blk', split_axis=1, concat_axis=0, tiled=True)  6.68 us
    unnamed x25, local copies, waits for them, and re-layouts  6.08 us
    all_to_all x1, starting transfers between devices, on_device(): lax.all_to_all(attended[:video_rows], 'blk', split_axis=0, concat_axis=1,...  5.64 us
    all_to_all x1, waiting for transfers between devices, on_device(): lax.all_to_all(q_norm, 'blk', split_axis=1, concat_axis=0, tiled=True)  4.72 us
  transfers between devices with their start and end apart: 4, of which 3 were waited for; matrix products, arithmetic and copies ran while one was open for 8% of the time, Pallas kernels for 0%

commit v1 on v0

--- a/solution.py
+++ b/solution.py
@@ -58,7 +58,10 @@
     rescale_factor = focus_sharpness[None, :, None] / math.sqrt(channel_width)
     q_norm = normed(footage_probes, footage_probes_amplitude, rescale_factor)
     k_norm = normed(footage_lookup_keys, footage_keys_amplitude, 1.0)
-    q_local = lax.all_to_all(q_norm, "blk", split_axis=1, concat_axis=0, tiled=True)
+    extra = lax.axis_size("blk")
+    odd = jnp.split(q_norm, extra, axis=1)
+    d_next = jnp.stack(odd)
+    q_local = jnp.concatenate(lax.all_to_all(d_next, "blk", 0, 0), 0)
     k_local = lax.all_to_all(k_norm, "blk", split_axis=1, concat_axis=0, tiled=True)
     v_local = lax.all_to_all(footage_payload, "blk", split_axis=1, concat_axis=0, tiled=True)
     local_heads = q_local.shape[1]

time: 77.5 us -> 77.1 us (level)
  waiting for transfers between devices: 18.5 us -> 17.2 us
    all_to_all x1, starting transfers between devices: 3.51 us -> 7.55 us  [on_device(): lax.all_to_all(k_norm, 'blk', split_axis=1, concat_axis=0, tiled=True)]
    all_to_all x1, starting transfers between devices: 7.41 us -> 3.51 us  [on_device(): q_local = jnp.concatenate(lax.all_to_all(d_next, 'blk', 0, 0), 0)]
    all_to_all x1, waiting for transfers between devices: 6.68 us -> 3.37 us  [on_device(): lax.all_to_all(k_norm, 'blk', split_axis=1, concat_axis=0, tiled=True)]
    all_to_all x1, waiting for transfers between devices: 4.72 us -> 6.7 us  [on_device(): q_local = jnp.concatenate(lax.all_to_all(d_next, 'blk', 0, 0), 0)]
    reduce_sum x3 -> x4, other arithmetic: 2.3 us -> 3.22 us  [normed(): jnp.mean(widened * widened, axis=-1, keepdims=True) + EPSILON]
    unnamed x25 -> x42, local copies, waits for them, and re-layouts: 6.08 us -> 6.48 us
  transfers between devices with their start and end apart: 4 -> 4, of which waited for: 3 -> 3; matrix products, arithmetic and copies ran while one was open for 8% -> 9% of each run, Pallas kernels for 0% -> 0%
where the time goes in v1:
time: 77.1 us; the launch traced here: 76.4 us
  starting transfers between devices  20.2 us (26%)
  blocking collectives  17.5 us (23%)
  waiting for transfers between devices  17.2 us (22%)
  local copies, waits for them, and re-layouts  7.82 us (10%)
  other arithmetic  6.69 us (9%)
  matrix products  5.96 us (8%)
  between operations  1.03 us (1%)
    all_gather x1, blocking collectives, on_device(): lax.all_gather(k_local, 'uly', axis=0, tiled=True)  9.16 us
    all_gather x1, blocking collectives, on_device(): lax.all_gather(v_local, 'uly', axis=0, tiled=True)  8.3 us
    all_to_all x1, starting transfers between devices, on_device(): lax.all_to_all(k_norm, 'blk', split_axis=1, concat_axis=0, tiled=True)  7.55 us
    all_to_all x1, waiting for transfers between devices, on_device(): lax.all_to_all(attended[:video_rows], 'blk', split_axis=0, concat_axis=1,...  7.13 us
    all_to_all x1, waiting for transfers between devices, on_device(): q_local = jnp.concatenate(lax.all_to_all(d_next, 'blk', 0, 0), 0)  6.7 us
    unnamed x42, local copies, waits for them, and re-layouts  6.48 us
    all_to_all x1, starting transfers between devices, on_device(): lax.all_to_all(attended[:video_rows], 'blk', split_axis=0, concat_axis=1,...  5.64 us
    all_to_all x1, starting transfers between devices, on_device(): q_local = jnp.concatenate(lax.all_to_all(d_next, 'blk', 0, 0), 0)  3.51 us
  transfers between devices with their start and end apart: 4, of which 3 were waited for; matrix products, arithmetic and copies ran while one was open for 9% of the time, Pallas kernels for 0%

profile of v1, /device:TPU:0, one launch (start us, length us, event | category | flops | bytes accessed | tf_op | source)
XLA Modules:
  0.0 76.4 jit_solution(10184962702147283171)
XLA Ops:
  0.6 0.0 copy-start
  0.6 0.0 copy-start.7
  0.7 0.0 copy-start.1
  0.7 0.0 copy-start.5
  0.7 1.3 %fusion.25 = f32[32,32]{0,1:T(8,128)S(1)} fusion(bf16[32,32,64]{2,1,0:T(8,128)(2,1)} %param.15), kind=kLoop, calls=%fused_computation.31 | loop fusion | flops 195584 | bytes 135168 | tf_op jit(solution)/shard_map/reduce_sum | solution.py:13
  1.9 0.1 copy.83
  2.0 0.1 copy.84
  2.1 1.2 %fusion.43 = bf16[32,32,64]{2,1,0:T(8,128)(2,1)S(1)} fusion(f32[64]{0:T(128)} %param.21, f32[32,32]{0,1:T(8,128)S(1)} %copy.84, bf16[32,32,64]{2,1,0:T(8,128)(2,1)} %param.15), kind=kLoop, calls=%fused_computation.94 | loop fusion | flops 262144 | bytes 266496
  3.3 0.9 %reshape.56 = bf16[16,2,2048]{2,1,0:T(2,128)(2,1)} reshape(bf16[32,32,64]{2,1,0:T(8,128)(2,1)S(1)} %fusion.43) | data formatting | bytes 262144
  4.2 0.0 copy-start.2
  4.2 7.5 %all-to-all-start.1 = ((bf16[16,2,2048]{2,1,0:T(2,128)(2,1)}), bf16[16,2,2048]{2,1,0:T(2,128)(2,1)S(1)}, u32[]{:S(2)}, u32[]{:S(2)}) async-start(bf16[16,2,2048]{2,1,0:T(2,128)(2,1)} %reshape.56), calls=%async_computation.1 | async-start | bytes 262144 | tf_op jit(solution)/shard_map/all_to_all | solution.py:65
  11.7 0.0 copy-done.7
  11.8 0.9 %multiply_reduce_fusion = f32[256,2]{0,1:T(2,128)S(1)} fusion(bf16[256,32,64]{0,2,1:T(8,128)(2,1)} %param.17, s32[]{:T(128)S(6)} %select_n.24), kind=kLoop, calls=%fused_computation.41 | loop fusion | flops 97792 | bytes 67588 | tf_op jit(solution)/shard_map/reduce_sum | solution.py:13
  12.6 0.0 copy-done.1
  12.7 0.2 fusion.21
  12.9 0.0 copy-done.5
  12.9 0.2 fusion.24
  13.1 0.0 copy-start.3
  13.2 0.0 copy-start.6
  13.6 0.9 %dynamic-slice_convert_fusion = f32[256,2,64]{0,2,1:T(8,128)S(1)} fusion(bf16[256,32,64]{0,2,1:T(8,128)(2,1)} %param.17, s32[]{:T(128)S(6)} %select_n.24), kind=kLoop, calls=%fused_computation.49 | loop fusion | flops 32768 | bytes 196612 | tf_op jit(solution)/shard_map/convert_element_type | solution.py:12
  14.5 0.9 %reshape.54 = bf16[16,2,2048]{2,1,0:T(2,128)(2,1)} reshape(bf16[16,32,2,64]{3,2,1,0:T(2,128)(2,1)S(1)} %constant_dynamic-update-slice_fusion) | data formatting | bytes 262144
  15.4 0.9 %fusion.28 = f32[256,2]{0,1:T(2,128)S(1)} fusion(bf16[256,32,64]{0,2,1:T(8,128)(2,1)} %param.18, s32[]{:T(128)S(6)} %select_n.24), kind=kLoop, calls=%fused_computation.38 | loop fusion | flops 97792 | bytes 67588 | tf_op jit(solution)/shard_map/reduce_sum | solution.py:13
  16.3 3.4 %all-to-all-done.1 = bf16[16,2,2048]{2,1,0:T(2,128)(2,1)S(1)} async-done(((bf16[16,2,2048]{2,1,0:T(2,128)(2,1)}), bf16[16,2,2048]{2,1,0:T(2,128)(2,1)S(1)}, u32[]{:S(2)}, u32[]{:S(2)}) %all-to-all-start.1) | async-done | bytes 131104 | tf_op jit(solution)/shard_map/all_to_all | solution.py:65
  19.6 3.5 %all-to-all-start = ((bf16[16,2,2048]{2,1,0:T(2,128)(2,1)}), bf16[16,2,2048]{2,1,0:T(2,128)(2,1)S(1)}, u32[]{:S(2)}, u32[]{:S(2)}) async-start(bf16[16,2,2048]{2,1,0:T(2,128)(2,1)} %reshape.54), calls=%async_computation | async-start | bytes 262144 | tf_op jit(solution)/shard_map/all_to_all | solution.py:64
  23.2 0.1 dynamic_slice.30
  23.2 0.0 copy-done.2
  23.3 0.1 copy.107
  23.4 0.9 %reshape.58 = bf16[16,2,2048]{2,1,0:T(2,128)(2,1)} reshape(bf16[32,32,64]{2,1,0:T(8,128)(2,1)S(1)} %bitcast.115) | data formatting | bytes 262144
  24.2 0.0 copy-done.3
  24.2 0.1 fusion.34
  24.3 6.7 %all-to-all-done = bf16[16,2,2048]{2,1,0:T(2,128)(2,1)S(1)} async-done(((bf16[16,2,2048]{2,1,0:T(2,128)(2,1)}), bf16[16,2,2048]{2,1,0:T(2,128)(2,1)S(1)}, u32[]{:S(2)}, u32[]{:S(2)}) %all-to-all-start) | async-done | bytes 131104 | tf_op jit(solution)/shard_map/all_to_all | solution.py:64
  31.0 3.5 %all-to-all-start.2 = ((bf16[16,2,2048]{2,1,0:T(2,128)(2,1)}), bf16[16,2,2048]{2,1,0:T(2,128)(2,1)S(1)}, u32[]{:S(2)}, u32[]{:S(2)}) async-start(bf16[16,2,2048]{2,1,0:T(2,128)(2,1)} %reshape.58), calls=%async_computation.2 | async-start | bytes 262144 | tf_op jit(solution)/shard_map/all_to_all | solution.py:66
  34.5 0.0 copy-done.6
  34.6 0.2 reshape.57
  34.8 9.2 %all_gather.6 = bf16[1024,2,64]{2,0,1:T(8,128)(2,1)S(1)} all-gather(bf16[512,2,64]{2,0,1:T(8,128)(2,1)S(1)} %bitcast.108), channel_id=1, replica_groups=mesh['blk'=16,'uly'=2] {'uly'}, dimensions={0}, use_global_device_ids=true | all-gather | bytes 393216 | tf_op jit(solution)/shard_map/all_gather | solution.py:109
  44.0 0.2 copy.88
  44.2 0.2 reshape.55
  44.4 0.1 copy.80
  44.5 0.0 all-to-all-done.2
  44.5 0.2 reshape.59
  44.8 0.0 copy-start.4
  44.8 8.3 %all_gather.7 = bf16[1024,2,64]{2,0,1:T(8,128)(2,1)S(1)} all-gather(bf16[512,2,64]{2,0,1:T(8,128)(2,1)S(1)} %bitcast.109), channel_id=1, replica_groups=mesh['blk'=16,'uly'=2] {'uly'}, dimensions={0}, use_global_device_ids=true | all-gather | bytes 393216 | tf_op jit(solution)/shard_map/all_gather | solution.py:110
  53.1 0.2 copy.89
  53.3 0.0 copy-done.4
  53.3 1.3 %fusion.42 = (f32[2,640]{1,0:T(2,128)S(1)}, f32[2,640,256]{1,2,0:T(8,128)S(1)}) fusion(f32[64]{0:T(128)S(1)} %copy-done.4, f32[256,2]{0,1:T(2,128)S(1)} %add_rsqrt_fusion.2, bf16[256,32,64]{0,2,1:T(8,128)(2,1)} %param.18, s32[]{:T(128)S(6)} %select_n.24, bf16[128,2,64]{0,2,1:T(8,128)(2,1)S(1)} %fusion.34, bf16[512,2,64]{0,2,1:T(8,128)(2,1)S(1)} %copy.80, ...), kind=kOutput, calls=%fused_computation.93 | convolution fusion | flops 43055872 | bytes 1547780 | tf_op jit(solution)/shard_map/qhd,khd->hqk/dot_general | solution.py:18
  54.6 0.3 fusion.17
  54.9 0.0 copy-done
  54.9 0.8 %fusion.16 = f32[2,640,64]{1,2,0:T(8,128)S(1)} fusion(f32[2,640,256]{1,2,0:T(8,128)S(1)} %get-tuple-element.195, f32[2,640]{1,0:T(2,128)S(1)} %get-tuple-element.252, pred[256]{0:T(512)(128)(4,1)S(1)} %broadcast_compare_fusion, bf16[256,32,64]{0,2,1:T(8,128)(2,1)S(1)} %copy-done, s32[]{:T(128)S(6)} %select_n.24), kind=kOutput, calls=%fused_computation.18 | convolution fusion | flops 252313600 | bytes 1709572 | tf_op jit(solution)/shard_map/hqk,khd->hqd/dot_general | solution.py:26
  55.7 4.7 %while.17 = (s32[]{:T(128)}, f32[2,640]{1,0:T(2,128)S(1)}, f32[2,640]{1,0:T(2,128)S(1)}, f32[2,640,64]{1,2,0:T(8,128)S(1)}, bf16[1024,2,64]{0,2,1:T(8,128)(2,1)S...) while((s32[]{:T(128)}, f32[2,640]{1,0:T(2,128)S(1)}, ...), condition=%wide.region_9.10_spmd, body=%wide.region_6.9_spmd.sunk | while | flops 590074880 | bytes 9017507 | solution.py:103
  55.8 0.6 bitcast_reduce_fusion.2
  56.3 0.4 fusion.53
  56.7 1.3 %fusion.54 = f32[2,640,64]{1,2,0:T(8,128)S(1)} fusion(f32[2,512,640]{2,1,0:T(8,128)S(1)} %get-tuple-element.245, f32[2,640]{1,0:T(2,128)S(1)} %get-tuple-element.246, f32[2,640,64]{1,2,0:T(8,128)S(1)} %get-tuple-element.265, f32[2,640]{1,0:T(2,128)S(1)} %get-tuple-element.249, f32[2,640]{1,0:T(2,128)S(1)} %get-tuple-element.250, ...), kind=kOutput, calls=%fused_computation.7.clone.1 | convolution fusion | flops 504217600 | bytes 3423236 | tf_op jit(solution)/shard_map/while/body/eval_jaxpr/hqk,khd->hqd/dot_general | solution.py:26
  58.1 0.6 bitcast_reduce_fusion.2
  58.7 0.4 fusion.53
  59.1 1.3 %fusion.54 = f32[2,640,64]{1,2,0:T(8,128)S(1)} fusion(f32[2,512,640]{2,1,0:T(8,128)S(1)} %get-tuple-element.245, f32[2,640]{1,0:T(2,128)S(1)} %get-tuple-element.246, f32[2,640,64]{1,2,0:T(8,128)S(1)} %get-tuple-element.265, f32[2,640]{1,0:T(2,128)S(1)} %get-tuple-element.249, f32[2,640]{1,0:T(2,128)S(1)} %get-tuple-element.250, ...), kind=kOutput, calls=%fused_computation.7.clone.1 | convolution fusion | flops 504217600 | bytes 3423236 | tf_op jit(solution)/shard_map/while/body/eval_jaxpr/hqk,khd->hqd/dot_general | solution.py:26
  60.5 0.2 copy.92
  60.7 0.2 slice.8
  60.9 0.9 %reshape.60 = bf16[16,2,2048]{2,1,0:T(2,128)(2,1)} reshape(bf16[512,2,64]{2,1,0:T(2,128)(2,1)S(1)} %slice.8) | data formatting | bytes 262144
  61.8 5.6 %all-to-all-start.3 = ((bf16[16,2,2048]{2,1,0:T(2,128)(2,1)}), bf16[16,2,2048]{2,1,0:T(2,128)(2,1)S(1)}, u32[]{:S(2)}, u32[]{:S(2)}) async-start(bf16[16,2,2048]{2,1,0:T(2,128)(2,1)} %reshape.60), calls=%async_computation.3 | async-start | bytes 262144 | tf_op jit(solution)/shard_map/all_to_all | solution.py:114
  67.5 0.7 copy.96
  68.2 7.1 %all-to-all-done.3 = bf16[16,2,2048]{2,1,0:T(2,128)(2,1)S(1)} async-done(((bf16[16,2,2048]{2,1,0:T(2,128)(2,1)}), bf16[16,2,2048]{2,1,0:T(2,128)(2,1)S(1)}, u32[]{:S(2)}, u32[]{:S(2)}) %all-to-all-start.3) | async-done | bytes 131104 | tf_op jit(solution)/shard_map/all_to_all | solution.py:114
  75.3 0.2 reshape.61
  75.6 0.8 %copy.95 = bf16[32,32,64]{2,1,0:T(8,128)(2,1)} copy(bf16[32,32,64]{2,0,1:T(8,128)(2,1)S(1)} %bitcast.114) | data formatting | bytes 262144
  (32 shorter events, 0.8 us)
Async XLA Ops:
  0.6 54.3 %copy-start = (bf16[256,32,64]{0,2,1:T(8,128)(2,1)S(1)}, bf16[256,32,64]{0,2,1:T(8,128)(2,1)}, u32[]{:S(2)}) copy-start(bf16[256,32,64]{0,2,1:T(8,128)(2,1)} %param.19) | copy-start | bytes 3145732
  0.6 11.1 %copy-start.7 = (f32[32]{0:T(128)S(1)}, f32[32]{0:T(128)}, u32[]{:S(2)}) copy-start(f32[32]{0:T(128)} %param.24) | copy-start | bytes 388
  0.7 12.0 %copy-start.1 = (bf16[32,32,64]{2,1,0:T(8,128)(2,1)S(1)}, bf16[32,32,64]{2,1,0:T(8,128)(2,1)}, u32[]{:S(2)}) copy-start(bf16[32,32,64]{2,1,0:T(8,128)(2,1)} %param.14) | copy-start | bytes 393220
  0.7 12.2 %copy-start.5 = (f32[64]{0:T(128)S(1)}, f32[64]{0:T(128)}, u32[]{:S(2)}) copy-start(f32[64]{0:T(128)} %param.20) | copy-start | bytes 772
  4.2 19.1 %copy-start.2 = (bf16[32,32,64]{2,1,0:T(8,128)(2,1)S(1)}, bf16[32,32,64]{2,1,0:T(8,128)(2,1)}, u32[]{:S(2)}) copy-start(bf16[32,32,64]{2,1,0:T(8,128)(2,1)} %param.16) | copy-start | bytes 393220
  4.2 15.5 %all-to-all-start.1 = ((bf16[16,2,2048]{2,1,0:T(2,128)(2,1)}), bf16[16,2,2048]{2,1,0:T(2,128)(2,1)S(1)}, u32[]{:S(2)}, u32[]{:S(2)}) async-start(bf16[16,2,2048]{2,1,0:T(2,128)(2,1)} %reshape.56), calls=%async_computation.1 | async-start | bytes 262144 | tf_op jit(solution)/shard_map/all_to_all | solution.py:65
  13.1 11.1 %copy-start.3 = (f32[64]{0:T(128)S(1)}, f32[64]{0:T(128)}, u32[]{:S(2)}) copy-start(f32[64]{0:T(128)} %param.22) | copy-start | bytes 772
  13.2 21.3 %copy-start.6 = (s32[256]{0:T(256)S(1)}, s32[256]{0:T(256)}, u32[]{:S(2)}) copy-start(s32[256]{0:T(256)} %param.25) | copy-start | bytes 3076
  19.6 11.4 %all-to-all-start = ((bf16[16,2,2048]{2,1,0:T(2,128)(2,1)}), bf16[16,2,2048]{2,1,0:T(2,128)(2,1)S(1)}, u32[]{:S(2)}, u32[]{:S(2)}) async-start(bf16[16,2,2048]{2,1,0:T(2,128)(2,1)} %reshape.54), calls=%async_computation | async-start | bytes 262144 | tf_op jit(solution)/shard_map/all_to_all | solution.py:64
  31.0 13.5 %all-to-all-start.2 = ((bf16[16,2,2048]{2,1,0:T(2,128)(2,1)}), bf16[16,2,2048]{2,1,0:T(2,128)(2,1)S(1)}, u32[]{:S(2)}, u32[]{:S(2)}) async-start(bf16[16,2,2048]{2,1,0:T(2,128)(2,1)} %reshape.58), calls=%async_computation.2 | async-start | bytes 262144 | tf_op jit(solution)/shard_map/all_to_all | solution.py:66
  44.8 8.6 %copy-start.4 = (f32[64]{0:T(128)S(1)}, f32[64]{0:T(128)}, u32[]{:S(2)}) copy-start(f32[64]{0:T(128)} %param.23) | copy-start | bytes 772
  61.8 13.6 %all-to-all-start.3 = ((bf16[16,2,2048]{2,1,0:T(2,128)(2,1)}), bf16[16,2,2048]{2,1,0:T(2,128)(2,1)S(1)}, u32[]{:S(2)}, u32[]{:S(2)}) async-start(bf16[16,2,2048]{2,1,0:T(2,128)(2,1)} %reshape.60), calls=%async_computation.3 | async-start | bytes 262144 | tf_op jit(solution)/shard_map/all_to_all | solution.py:114
